TPU v7x, 128 devices: a whole 4x4x4 slice. The times are simulated.
128 devices in a mesh: lat: 8 (over x, core), lon: 16 (over z, y).
Axes of the slice: x: 4, y: 4, z: 4, core: 2. Of those that a mesh axis runs over, the one named last changes fastest.
Arguments:
- tracers: bfloat16 [512, 2048, 32, 4], P('lat', 'lon'), may hold values from 0 to 2
- weights: bfloat16 [512, 16, 8, 128, 128], P('lat', 'lon'), may hold values from -1 to 1, as said below
- source_row: int32 [512, 16, 8], P('lat', 'lon'), may hold values from 0 to 511, as said below
- source_block: int32 [512, 16, 8], P('lat', 'lon'), may hold values from 0 to 15, as said below
- slot_count: int32 [512, 16], P('lat', 'lon'), may hold values from 1 to 8, as said below
Outputs:
- advected_fixed: float32 [512, 2048, 32, 4], P('lat', 'lon')
Inputs may be any that keep to these rules, and one draw needn't show every extreme that they name: source_row differs from the target tile's own row by at most 4 and lies within the grid. source_block lies at cyclic distance at most 2 from the target tile's own index along the row, except for target tiles of the first and the last latitude row, where it may reach 3; the allowed distance grows from 1 at the equator towards the poles; in the two outermost rows slot 0 reaches exactly 3 sectors ahead on even tiles and 3 sectors behind on odd tiles. slot_count grows from 1 or 2 at the equator to 8 at the two outermost rows. weights are of either sign; for each target tile the weights of each target cell over the used slots and all source cells sum (before rounding to bfloat16) to one value of that tile between 0.9 and 1.05.
All inputs are finite; a program needn't handle non-finite values.
Results may differ from a plain program's by a relative error of at most 0.0003.
Values may be sent and summed in bfloat16 or wider, within the bound.
No kernel may reach another device: no remote copies, remote signals or barrier semaphores. Data moves between devices by JAX's collectives and lax.ppermute only.
A program may use at most 192 MiB of HBM per device.

v0:
```python
import math
import jax
import jax.numpy as jnp
from jax import lax
from jax.sharding import Mesh
from jax.sharding import PartitionSpec as P

RLAT = 4
REACH = 3
LAT = ("lat_0", "lat_1")
LON = ("lon_0", "lon_1")
LAT_LON = ("lat_0", "lat_1", "lon_0", "lon_1")


def extended(value, sides, width):
    for axis, dim in sides:
        size, length = (lax.axis_size(axis), value.shape[dim])
        up = [(i, (i + 1) % size) for i in range(size - 1)]
        down = [(j, i) for i, j in up]
        last = lax.slice_in_dim(value, length - width, length, axis=dim)
        leading = lax.slice_in_dim(value, 0, width, axis=dim)
        before = lax.ppermute(last, axis, up)
        after = lax.ppermute(leading, axis, down)
        value = jnp.concatenate([before, value, after], axis=dim)
    return value


def shifted(value, axis, by):
    length = lax.axis_size(axis)
    return lax.ppermute(value, axis, [(i, (i + by) % length) for i in range(length)])


def by_axis(value, axes):
    for axis in axes:
        value = lax.psum(value, axis)
    return value


def latitude_area(total_rows, first_row, count_rows):
    rows_all = jnp.arange(count_rows, dtype=jnp.int32) + first_row
    angle = -0.5 * math.pi + (rows_all.astype(jnp.float32) + 0.5) * (math.pi / total_rows)
    return jnp.cos(angle)


def local(tracers, weights, source_row, source_block, slot_count):
    rows_dev, tile_width, levels, tracer_kinds = tracers.shape
    channels = levels * tracer_kinds
    lat_count = lax.axis_size(LAT)
    lon_count = lax.axis_size(LON)
    lat_index = lax.axis_index(LAT)
    lon_index = lax.axis_index(LON)
    field = tracers.reshape(rows_dev, tile_width, channels)
    total_rows = rows_dev * lat_count
    area = latitude_area(total_rows, lat_index * rows_dev, rows_dev)
    total_area = tile_width * lon_count * jnp.sum(latitude_area(total_rows, 0, total_rows))
    mass_old = jnp.sum(area[:, None, None] * field, axis=(0, 1))
    padded = extended(field, ((LAT, 0),), RLAT)
    local_row = source_row[:, 0, :] - (lat_index * rows_dev - RLAT)
    wanted = source_block[:, 0, :]
    slots_max = source_row.shape[2]
    relative = (wanted - lon_index + REACH) % lon_count - REACH
    near_list = []
    for distance in range(-(REACH - 1), REACH):
        if distance == 0:
            near_list.append(padded)
        else:
            near_list.append(shifted(padded, LON, -distance))
    near_stack = jnp.stack(near_list, axis=1)
    near_pick = near_stack[local_row, jnp.clip(relative + REACH - 1, 0, 2 * REACH - 2)]
    polar_slab = jnp.concatenate(
        [padded[RLAT : 2 * RLAT + 1], padded[rows_dev - 1 : rows_dev + RLAT]], axis=0
    )
    far_list = [shifted(polar_slab, LON, -distance) for distance in (-REACH, REACH)]
    upper = (jnp.arange(rows_dev, dtype=jnp.int32) < rows_dev // 2)[:, None]
    far_row = jnp.where(upper, local_row - RLAT, local_row - (rows_dev - 1) + RLAT + 1)
    far_row = jnp.clip(far_row, 0, 2 * RLAT + 1)
    far_stack = jnp.stack(far_list, axis=1)
    far_pick = far_stack[
        jnp.clip(far_row, 0, far_stack.shape[0] - 1), (relative > 0).astype(jnp.int32)
    ]
    active = jnp.arange(slots_max, dtype=jnp.int32)[None, :] < slot_count
    is_far = jnp.abs(relative) == REACH
    picked = jnp.where(
        (active & is_far)[:, :, None, None],
        far_pick,
        jnp.where(active[:, :, None, None], near_pick, jnp.zeros((), near_pick.dtype)),
    )
    advected = jnp.einsum(
        "tkij,tkjc->tic", weights[:, 0], picked, preferred_element_type=jnp.float32
    )
    mass_new = jnp.sum(area[:, None, None] * advected, axis=(0, 1))
    summed_old, summed_new = (by_axis(mass_old, LAT_LON), by_axis(mass_new, LAT_LON))
    fixed = advected + (summed_old - summed_new) / total_area
    return fixed.reshape(rows_dev, tile_width, levels, tracer_kinds)


def solution(mesh):
    finer = Mesh(mesh.devices.reshape(4, 2, 4, 4), ("lat_0", "lat_1", "lon_0", "lon_1"))
    placed = (
        P(LAT, LON, None, None),
        P(LAT, LON, None, None, None),
        P(LAT, LON, None),
        P(LAT, LON, None),
        P(LAT, LON),
    )
    return jax.shard_map(
        local, mesh=finer, in_specs=placed, out_specs=P(LAT, LON, None, None), check_vma=False
    )
```

profile of v0, /device:TPU:0, one launch (start us, length us, event | category | flops | bytes accessed | tf_op | source)
XLA Modules:
  0.0 289.7 jit_solution(14839024553744103163)
XLA Ops:
  0.0 0.0 copy-start
  0.0 1.2 fusion.28
  1.2 1.3 collective-permute-start.2
  2.5 1.3 collective-permute-start.3
  3.8 0.0 collective-permute-done.2
  3.8 3.8 %collective-permute-done.3 = bf16[4,128,128]{1,2,0:T(8,128)(2,1)S(1)} collective-permute-done((bf16[4,128,128]{1,2,0:T(8,128)(2,1)S(1)}, bf16[4,128,128]{1,2,0:T(8,128)(2,1)S(1)}, u32[]{:S(2)}, u32[]{:S(2)}) %collective-permute-start.3) | collective-permute-done | bytes 131104 | tf_op jit(solution)/shard_map/ppermute | solution.py:23
  7.6 3.3 %pad_maximum_fusion = bf16[72,128,128]{1,2,0:T(8,128)(2,1)} fusion(bf16[4,128,128]{1,2,0:T(8,128)(2,1)S(1)} %collective-permute-done.3, bf16[64,128,128]{1,2,0:T(8,128)(2,1)} %bitcast.64, bf16[4,128,128]{1,2,0:T(8,128)(2,1)S(1)} %collective-permute-done.2), kind=kLoop, calls=%fused_computation.13 | loop fusion | flops 2359296 | bytes 4718592 | tf_op jit(solution)/shard_map/concatenate | solution.py:24
  10.9 3.2 %collective-permute-start.4 = (bf16[72,128,128]{1,2,0:T(8,128)(2,1)}, bf16[72,128,128]{1,2,0:T(8,128)(2,1)}, u32[]{:S(2)}, u32[]{:S(2)}) collective-permute-start(bf16[72,128,128]{1,2,0:T(8,128)(2,1)} %pad_maximum_fusion), channel_id=1, source_target_pairs={{0,2},{1,3},{2,4},{3,5},{4,6},{5,7},{6,8},{7,9},{8,10},{9,11},{10,... | collective-permute-start | bytes 7077896 | tf_op jit(solution)/shard_map/ppermute | solution.py:30
  14.1 0.7 collective-permute-start.5
  14.8 4.7 %collective-permute-start.6 = (bf16[72,128,128]{1,2,0:T(8,128)(2,1)}, bf16[72,128,128]{1,2,0:T(8,128)(2,1)}, u32[]{:S(2)}, u32[]{:S(2)}) collective-permute-start(bf16[72,128,128]{1,2,0:T(8,128)(2,1)} %pad_maximum_fusion), channel_id=1, source_target_pairs={{0,15},{1,0},{2,1},{3,2},{4,3},{5,4},{6,5},{7,6},{8,7},{9,8},{10,9... | collective-permute-start | bytes 7077896 | tf_op jit(solution)/shard_map/ppermute | solution.py:30
  19.4 0.0 copy-done
  19.4 0.1 fusion.29
  19.6 0.9 collective-permute-start.7
  20.6 0.1 collective-permute-start
  20.7 0.0 copy-done.2
  20.7 0.0 copy-done.4
  20.7 0.0 copy-done.3
  20.7 155.5 %collective-permute-done = bf16[10,128,128]{1,2,0:T(8,128)(2,1)S(1)} collective-permute-done((bf16[10,128,128]{1,2,0:T(8,128)(2,1)S(1)}, bf16[10,128,128]{1,2,0:T(8,128)(2,1)S(1)}, u32[]{:S(2)}, u32[]{:S(2)}) %collective-permute-start) | collective-permute-done | bytes 327712 | tf_op jit(solution)/shard_map/ppermute | solution.py:30
  176.2 4.5 %collective-permute-start.1 = (bf16[10,128,128]{1,2,0:T(8,128)(2,1)S(1)}, bf16[10,128,128]{1,2,0:T(8,128)(2,1)S(1)}, u32[]{:S(2)}, u32[]{:S(2)}) collective-permute-start(bf16[10,128,128]{1,2,0:T(8,128)(2,1)S(1)} %pad_maximum_fusion.2), channel_id=1, source_target_pairs={{0,13},{1,14},{2,15},{3,0},{4,1},{5,2},{6,3},{7,4},{8,5},{9,6},{10... | collective-permute-start | bytes 983048 | tf_op jit(solution)/shard_map/ppermute | solution.py:30
  180.8 0.1 copy.11
  180.9 0.1 reshape.258
  181.0 0.1 copy.9
  181.0 0.1 reshape.252
  181.1 0.1 copy.10
  181.2 0.1 copy.8
  181.3 1.4 multiply_reduce_fusion
  182.7 0.1 reduce_sum.30
  182.8 0.7 cosine_reduce_fusion
  184.1 3.8 %collective-permute-done.1 = bf16[10,128,128]{1,2,0:T(8,128)(2,1)S(1)} collective-permute-done((bf16[10,128,128]{1,2,0:T(8,128)(2,1)S(1)}, bf16[10,128,128]{1,2,0:T(8,128)(2,1)S(1)}, u32[]{:S(2)}, u32[]{:S(2)}) %collective-permute-start.1) | collective-permute-done | bytes 327712 | tf_op jit(solution)/shard_map/ppermute | solution.py:30
  188.0 0.7 copy-done.1
  188.7 1.0 pad_maximum_fusion.1
  189.7 10.8 %gather_fusion = bf16[512,128,128]{1,2,0:T(8,128)(2,1)} fusion(bf16[10,2,128,128]{2,3,0,1:T(8,128)(2,1)S(1)} %pad_maximum_fusion.1, s32[512]{0:T(512)S(1)} %reshape.252), kind=kCustom, calls=%fused_computation | custom fusion | bytes 33558528 | tf_op jit(solution)/shard_map/gather | solution.py:78
  200.5 0.0 collective-permute-done.4
  200.5 3.3 %bitcast_dynamic-update-slice_fusion.4 = bf16[72,5,128,128]{2,3,0,1:T(8,128)(2,1)} fusion(bf16[72,128,128]{1,2,0:T(8,128)(2,1)} %collective-permute-done.4), kind=kLoop, calls=%fused_computation.18 | loop fusion | bytes 4718592
  203.9 0.0 collective-permute-done.5
  203.9 3.4 %bitcast_dynamic-update-slice_fusion.3 = bf16[72,5,128,128]{2,3,0,1:T(8,128)(2,1)} fusion(bf16[72,5,128,128]{2,3,0,1:T(8,128)(2,1)} %bitcast_dynamic-update-slice_fusion.4, bf16[72,128,128]{1,2,0:T(8,128)(2,1)} %collective-permute-done.5), kind=kLoop, calls=%fused_computation.17 | loop fusion | bytes 4718592
  207.3 1.6 bitcast_dynamic-update-slice_fusion.2
  208.8 0.0 collective-permute-done.6
  208.8 3.4 %bitcast_dynamic-update-slice_fusion.1 = bf16[72,5,128,128]{2,3,0,1:T(8,128)(2,1)} fusion(bf16[72,5,128,128]{2,3,0,1:T(8,128)(2,1)} %bitcast_dynamic-update-slice_fusion.2, bf16[72,128,128]{1,2,0:T(8,128)(2,1)} %collective-permute-done.6), kind=kLoop, calls=%fused_computation.15 | loop fusion | bytes 4718592
  212.2 0.0 collective-permute-done.7
  212.2 3.4 %bitcast_dynamic-update-slice_fusion = bf16[72,5,128,128]{2,3,0,1:T(8,128)(2,1)} fusion(bf16[72,5,128,128]{2,3,0,1:T(8,128)(2,1)} %bitcast_dynamic-update-slice_fusion.1, bf16[72,128,128]{1,2,0:T(8,128)(2,1)} %collective-permute-done.7), kind=kLoop, calls=%fused_computation.14 | loop fusion | bytes 4718592 | tf_op jit(solution)/shard_map/stack | solution.py:68
  215.6 15.2 %gather_fusion.1 = bf16[512,128,128]{1,2,0:T(8,128)(2,1)} fusion(bf16[72,5,128,128]{2,3,0,1:T(8,128)(2,1)} %bitcast_dynamic-update-slice_fusion, s32[512]{0:T(512)S(1)} %reshape.258), kind=kCustom, calls=%fused_computation.1 | custom fusion | bytes 33558528 | tf_op jit(solution)/shard_map/gather | solution.py:69
  230.7 19.4 %fusion.7 = (f32[128]{0:T(128)S(1)}, f32[64,128,128,1]{2,1,3,0:T(8,128)}) fusion(f32[64]{0:T(128)S(1)} %add_cosine_fusion, bf16[64,1,8,128,128]{4,3,2,1,0:T(8,128)(2,1)} %param.6, bf16[64,8,128,128]{2,3,1,0:T(8,128)(2,1)} %bitcast.66, bf16[64,8,128,128]{2,3,1,0:T(8,128)(2,1)} %bitcast.67, pred[64,8]{1,0:T(8,128)(4,1)S(1)} %copy.10, pred[64,8]{1,0:T(8,128)(4,1)S(1)} %copy.8), kind=kOutput, calls=%fused_computation.11 | convolution fusion | flops 2166358016 | bytes 54527744 | tf_op jit(solution)/shard_map/tkij,tkjc->tic/dot_general | solution.py:88
  250.2 12.5 %all-reduce.2 = (f32[128]{0:T(128)S(1)}, f32[128]{0:T(128)S(1)}) all-reduce(f32[128]{0:T(128)S(1)} %reduce_sum.30, f32[128]{0:T(128)S(1)} %get-tuple-element.21), channel_id=1, replica_groups=mesh['lat_0'=4,'lat_1'=2,'lon_0'=4,'lon_1'=4] {'lat_0'}, use_global_device_ids=true, to_apply=%region_1.0 | all-reduce | flops 256 | bytes 2048 | tf_op jit(solution)/shard_map/psum | solution.py:35
  262.6 2.5 all-reduce.3
  265.1 8.2 %all-reduce.1 = (f32[128]{0:T(128)S(1)}, f32[128]{0:T(128)S(1)}) all-reduce(f32[128]{0:T(128)S(1)} %get-tuple-element.11, f32[128]{0:T(128)S(1)} %get-tuple-element.12), channel_id=1, replica_groups=mesh['lat_0'=4,'lat_1'=2,'lon_0'=4,'lon_1'=4] {'lon_0'}, use_global_device_ids=true, to_apply=%region_3.4 | all-reduce | flops 256 | bytes 2048 | tf_op jit(solution)/shard_map/psum | solution.py:35
  273.3 11.6 %all-reduce = (f32[128]{0:T(128)S(1)}, f32[128]{0:T(128)S(1)}) all-reduce(f32[128]{0:T(128)S(1)} %get-tuple-element.7, f32[128]{0:T(128)S(1)} %get-tuple-element.8), channel_id=1, replica_groups=mesh['lat_0'=4,'lat_1'=2,'lon_0'=4,'lon_1'=4] {'lon_1'}, use_global_device_ids=true, to_apply=%region_4.5 | all-reduce | flops 256 | bytes 2048 | tf_op jit(solution)/shard_map/psum | solution.py:35
  284.8 4.9 %bitcast_add_fusion = f32[64,128,128]{2,1,0:T(8,128)} fusion(f32[64,128,128,1]{2,1,3,0:T(8,128)} %get-tuple-element.22, f32[128]{0:T(128)S(1)} %subtract_divide_fusion), kind=kLoop, calls=%fused_computation.9 | loop fusion | flops 1048576 | bytes 8389120 | tf_op jit(solution)/shard_map/add | solution.py:93
  (10 shorter events, 0.1 us)
Async XLA Ops:
  0.0 19.4 %copy-start = (bf16[64,128,32,4]{1,3,2,0:T(4,128)(2,1)S(1)}, bf16[64,128,32,4]{1,3,2,0:T(4,128)(2,1)}, u32[]{:S(2)}) copy-start(bf16[64,128,32,4]{1,3,2,0:T(4,128)(2,1)} %param.5) | copy-start | bytes 6291460
  0.0 20.7 %copy-start.2 = (s32[64,1,8]{0,2,1:T(8,128)S(1)}, s32[64,1,8]{0,2,1:T(8,128)}, u32[]{:S(2)}) copy-start(s32[64,1,8]{0,2,1:T(8,128)} %param.8) | copy-start | bytes 6148
  0.0 20.7 %copy-start.4 = (s32[64,1]{0,1:T(1,128)S(1)}, s32[64,1]{0,1:T(1,128)}, u32[]{:S(2)}) copy-start(s32[64,1]{0,1:T(1,128)} %param.9) | copy-start | bytes 772
  0.0 20.7 %copy-start.3 = (s32[64,1,8]{0,2,1:T(8,128)S(1)}, s32[64,1,8]{0,2,1:T(8,128)}, u32[]{:S(2)}) copy-start(s32[64,1,8]{0,2,1:T(8,128)} %param.7) | copy-start | bytes 6148
  1.2 2.6 collective-permute-start.2
  2.5 5.1 %collective-permute-start.3 = (bf16[4,128,128]{1,2,0:T(8,128)(2,1)S(1)}, bf16[4,128,128]{1,2,0:T(8,128)(2,1)S(1)}, u32[]{:S(2)}, u32[]{:S(2)}) collective-permute-start(bf16[4,128,128]{1,2,0:T(8,128)(2,1)S(1)} %bitcast.72), channel_id=1, source_target_pairs={{16,0},{32,16},{48,32},{64,48},{80,64},{96,80},{112,96},{17,1},{33... | collective-permute-start | bytes 393224 | tf_op jit(solution)/shard_map/ppermute | solution.py:23
  10.9 189.6 %collective-permute-start.4 = (bf16[72,128,128]{1,2,0:T(8,128)(2,1)}, bf16[72,128,128]{1,2,0:T(8,128)(2,1)}, u32[]{:S(2)}, u32[]{:S(2)}) collective-permute-start(bf16[72,128,128]{1,2,0:T(8,128)(2,1)} %pad_maximum_fusion), channel_id=1, source_target_pairs={{0,2},{1,3},{2,4},{3,5},{4,6},{5,7},{6,8},{7,9},{8,10},{9,11},{10,... | collective-permute-start | bytes 7077896 | tf_op jit(solution)/shard_map/ppermute | solution.py:30
  14.1 189.8 %collective-permute-start.5 = (bf16[72,128,128]{1,2,0:T(8,128)(2,1)}, bf16[72,128,128]{1,2,0:T(8,128)(2,1)}, u32[]{:S(2)}, u32[]{:S(2)}) collective-permute-start(bf16[72,128,128]{1,2,0:T(8,128)(2,1)} %pad_maximum_fusion), channel_id=1, source_target_pairs={{0,1},{1,2},{2,3},{3,4},{4,5},{5,6},{6,7},{7,8},{8,9},{9,10},{10,1... | collective-permute-start | bytes 7077896 | tf_op jit(solution)/shard_map/ppermute | solution.py:30
  14.8 194.1 %collective-permute-start.6 = (bf16[72,128,128]{1,2,0:T(8,128)(2,1)}, bf16[72,128,128]{1,2,0:T(8,128)(2,1)}, u32[]{:S(2)}, u32[]{:S(2)}) collective-permute-start(bf16[72,128,128]{1,2,0:T(8,128)(2,1)} %pad_maximum_fusion), channel_id=1, source_target_pairs={{0,15},{1,0},{2,1},{3,2},{4,3},{5,4},{6,5},{7,6},{8,7},{9,8},{10,9... | collective-permute-start | bytes 7077896 | tf_op jit(solution)/shard_map/ppermute | solution.py:30
  19.6 192.6 %collective-permute-start.7 = (bf16[72,128,128]{1,2,0:T(8,128)(2,1)}, bf16[72,128,128]{1,2,0:T(8,128)(2,1)}, u32[]{:S(2)}, u32[]{:S(2)}) collective-permute-start(bf16[72,128,128]{1,2,0:T(8,128)(2,1)} %pad_maximum_fusion), channel_id=1, source_target_pairs={{0,14},{1,15},{2,0},{3,1},{4,2},{5,3},{6,4},{7,5},{8,6},{9,7},{10,... | collective-permute-start | bytes 7077896 | tf_op jit(solution)/shard_map/ppermute | solution.py:30
  20.6 155.7 %collective-permute-start = (bf16[10,128,128]{1,2,0:T(8,128)(2,1)S(1)}, bf16[10,128,128]{1,2,0:T(8,128)(2,1)S(1)}, u32[]{:S(2)}, u32[]{:S(2)}) collective-permute-start(bf16[10,128,128]{1,2,0:T(8,128)(2,1)S(1)} %pad_maximum_fusion.2), channel_id=1, source_target_pairs={{0,3},{1,4},{2,5},{3,6},{4,7},{5,8},{6,9},{7,10},{8,11},{9,12},{10... | collective-permute-start | bytes 983048 | tf_op jit(solution)/shard_map/ppermute | solution.py:30
  176.2 11.8 %collective-permute-start.1 = (bf16[10,128,128]{1,2,0:T(8,128)(2,1)S(1)}, bf16[10,128,128]{1,2,0:T(8,128)(2,1)S(1)}, u32[]{:S(2)}, u32[]{:S(2)}) collective-permute-start(bf16[10,128,128]{1,2,0:T(8,128)(2,1)S(1)} %pad_maximum_fusion.2), channel_id=1, source_target_pairs={{0,13},{1,14},{2,15},{3,0},{4,1},{5,2},{6,3},{7,4},{8,5},{9,6},{10... | collective-permute-start | bytes 983048 | tf_op jit(solution)/shard_map/ppermute | solution.py:30
  188.0 0.7 copy-start.1
where the time goes:
time: 290 us
  waiting for transfers between devices  163 us (56%)
  local copies, waits for them, and re-layouts  42.2 us (15%)
  blocking collectives  34.6 us (12%)
  matrix products  19.4 us (7%)
  starting transfers between devices  16.7 us (6%)
  other arithmetic  13 us (4%)
    ppermute x6, waiting for transfers between devices, shifted(): lax.ppermute(value, axis, [(i, (i + by) % length) for i in range(length)])  159 us
    psum x4, blocking collectives, by_axis(): value = lax.psum(value, axis)  34.6 us
    dot_general x1, matrix products, local(): jnp.einsum('tkij,tkjc->tic', weights[:, 0], picked, preferred_element_typ...  19.4 us
    gather x1, local copies, waits for them, and re-layouts, local(): near_stack[local_row, jnp.clip(relative + REACH - 1, 0, 2 * REACH - 2)]  15.2 us
    ppermute x6, starting transfers between devices, shifted(): lax.ppermute(value, axis, [(i, (i + by) % length) for i in range(length)])  14.1 us
    unnamed x13, local copies, waits for them, and re-layouts  10.9 us
    gather x1, local copies, waits for them, and re-layouts, local(): far_stack[jnp.clip(far_row, 0, far_stack.shape[0] - 1), (relative > 0).as...  10.8 us
  transfers between devices with their start and end apart: 8, of which 3 were waited for; matrix products, arithmetic and copies ran while one was open for 9% of the time, Pallas kernels for 0%

commit v1 on v0

--- a/solution.py
+++ b/solution.py
@@ -32,7 +32,7 @@
 
 def by_axis(value, axes):
     for axis in axes:
-        value = lax.psum(value, axis)
+        value = jnp.sum(lax.all_gather(value, axis), axis=0)
     return value
 
 

time: 290 us -> 306 us (1.055)
  blocking collectives: 34.6 us -> 53.7 us
  waiting for transfers between devices: 163 us -> 159 us
    all_gather x0 -> x8, blocking collectives: none -> 53.7 us  [by_axis(): value = jnp.sum(lax.all_gather(value, axis), axis=0)]
    psum x4 -> x0, blocking collectives: 34.6 us -> none  [by_axis(): value = lax.psum(value, axis)]
    ppermute x6, waiting for transfers between devices: 159 us -> 155 us  [shifted(): lax.ppermute(value, axis, [(i, (i + by) % length) for i in range(length)])]
    unnamed x13 -> x14, local copies, waits for them, and re-layouts: 10.9 us -> 11 us
  transfers between devices with their start and end apart: 8 -> 8, of which waited for: 3 -> 2; matrix products, arithmetic and copies ran while one was open for 9% -> 9% of each run, Pallas kernels for 0% -> 0%
where the time goes in v1:
time: 306 us; the launch traced here: 305 us
  waiting for transfers between devices  159 us (52%)
  blocking collectives  53.7 us (18%)
  local copies, waits for them, and re-layouts  42.2 us (14%)
  matrix products  19.4 us (6%)
  starting transfers between devices  16.7 us (5%)
  other arithmetic  13.3 us (4%)
    ppermute x6, waiting for transfers between devices, shifted(): lax.ppermute(value, axis, [(i, (i + by) % length) for i in range(length)])  155 us
    all_gather x8, blocking collectives, by_axis(): value = jnp.sum(lax.all_gather(value, axis), axis=0)  53.7 us
    dot_general x1, matrix products, local(): jnp.einsum('tkij,tkjc->tic', weights[:, 0], picked, preferred_element_typ...  19.4 us
    gather x1, local copies, waits for them, and re-layouts, local(): near_stack[local_row, jnp.clip(relative + REACH - 1, 0, 2 * REACH - 2)]  15.2 us
    ppermute x6, starting transfers between devices, shifted(): lax.ppermute(value, axis, [(i, (i + by) % length) for i in range(length)])  14.1 us
    unnamed x14, local copies, waits for them, and re-layouts  11 us
    gather x1, local copies, waits for them, and re-layouts, local(): far_stack[jnp.clip(far_row, 0, far_stack.shape[0] - 1), (relative > 0).as...  10.8 us
  transfers between devices with their start and end apart: 8, of which 2 were waited for; matrix products, arithmetic and copies ran while one was open for 9% of the time, Pallas kernels for 0%

profile of v1, /device:TPU:0, one launch (start us, length us, event | category | flops | bytes accessed | tf_op | source)
XLA Modules:
  0.0 305.4 jit_solution(10397597126511674741)
XLA Ops:
  0.0 1.2 fusion.28
  1.2 1.3 collective-permute-start.2
  2.5 1.3 collective-permute-start.3
  3.8 0.0 collective-permute-done.2
  3.8 3.8 %collective-permute-done.3 = bf16[4,128,128]{1,2,0:T(8,128)(2,1)S(1)} collective-permute-done((bf16[4,128,128]{1,2,0:T(8,128)(2,1)S(1)}, bf16[4,128,128]{1,2,0:T(8,128)(2,1)S(1)}, u32[]{:S(2)}, u32[]{:S(2)}) %collective-permute-start.3) | collective-permute-done | bytes 131104 | tf_op jit(solution)/shard_map/ppermute | solution.py:23
  7.6 3.3 %pad_maximum_fusion = bf16[72,128,128]{1,2,0:T(8,128)(2,1)} fusion(bf16[4,128,128]{1,2,0:T(8,128)(2,1)S(1)} %collective-permute-done.3, bf16[64,128,128]{1,2,0:T(8,128)(2,1)} %bitcast.71, bf16[4,128,128]{1,2,0:T(8,128)(2,1)S(1)} %collective-permute-done.2), kind=kLoop, calls=%fused_computation.13 | loop fusion | flops 2359296 | bytes 4718592 | tf_op jit(solution)/shard_map/concatenate | solution.py:24
  10.9 3.2 %collective-permute-start.4 = (bf16[72,128,128]{1,2,0:T(8,128)(2,1)}, bf16[72,128,128]{1,2,0:T(8,128)(2,1)}, u32[]{:S(2)}, u32[]{:S(2)}) collective-permute-start(bf16[72,128,128]{1,2,0:T(8,128)(2,1)} %pad_maximum_fusion), channel_id=1, source_target_pairs={{0,2},{1,3},{2,4},{3,5},{4,6},{5,7},{6,8},{7,9},{8,10},{9,11},{10,... | collective-permute-start | bytes 7077896 | tf_op jit(solution)/shard_map/ppermute | solution.py:30
  14.1 0.7 collective-permute-start.5
  14.8 4.7 %collective-permute-start.6 = (bf16[72,128,128]{1,2,0:T(8,128)(2,1)}, bf16[72,128,128]{1,2,0:T(8,128)(2,1)}, u32[]{:S(2)}, u32[]{:S(2)}) collective-permute-start(bf16[72,128,128]{1,2,0:T(8,128)(2,1)} %pad_maximum_fusion), channel_id=1, source_target_pairs={{0,15},{1,0},{2,1},{3,2},{4,3},{5,4},{6,5},{7,6},{8,7},{9,8},{10,9... | collective-permute-start | bytes 7077896 | tf_op jit(solution)/shard_map/ppermute | solution.py:30
  19.4 0.0 copy-done
  19.4 0.1 fusion.29
  19.6 0.9 collective-permute-start.7
  20.6 0.1 collective-permute-start
  20.7 155.5 %collective-permute-done = bf16[10,128,128]{1,2,0:T(8,128)(2,1)S(1)} collective-permute-done((bf16[10,128,128]{1,2,0:T(8,128)(2,1)S(1)}, bf16[10,128,128]{1,2,0:T(8,128)(2,1)S(1)}, u32[]{:S(2)}, u32[]{:S(2)}) %collective-permute-start) | collective-permute-done | bytes 327712 | tf_op jit(solution)/shard_map/ppermute | solution.py:30
  176.2 4.5 %collective-permute-start.1 = (bf16[10,128,128]{1,2,0:T(8,128)(2,1)S(1)}, bf16[10,128,128]{1,2,0:T(8,128)(2,1)S(1)}, u32[]{:S(2)}, u32[]{:S(2)}) collective-permute-start(bf16[10,128,128]{1,2,0:T(8,128)(2,1)S(1)} %pad_maximum_fusion.2), channel_id=1, source_target_pairs={{0,13},{1,14},{2,15},{3,0},{4,1},{5,2},{6,3},{7,4},{8,5},{9,6},{10... | collective-permute-start | bytes 983048 | tf_op jit(solution)/shard_map/ppermute | solution.py:30
  180.8 0.1 copy.15
  180.9 0.1 reshape.264
  181.0 0.1 copy.13
  181.0 0.1 reshape.258
  181.1 0.1 copy.12
  181.2 0.1 copy.14
  181.3 1.4 multiply_reduce_fusion
  182.7 0.1 reshape.277
  182.8 10.3 %all-gather.7 = f32[4,1,128]{2,1,0:T(1,128)S(1)} all-gather(f32[1,1,128]{2,1,0:T(1,128)S(1)} %reshape.277), channel_id=1, replica_groups=mesh['lat_0'=4,'lat_1'=2,'lon_0'=4,'lon_1'=4] {'lat_0'}, dimensions={0}, use_global_device_ids=true | all-gather | bytes 2560 | tf_op jit(solution)/shard_map/all_gather | solution.py:35
  193.2 1.8 all-gather.8
  195.0 7.4 %all-gather.9 = f32[4,1,128]{2,1,0:T(1,128)S(1)} all-gather(f32[1,1,128]{2,1,0:T(1,128)S(1)} %bitcast.81), channel_id=3, replica_groups=mesh['lat_0'=4,'lat_1'=2,'lon_0'=4,'lon_1'=4] {'lon_0'}, dimensions={0}, use_global_device_ids=true | all-gather | bytes 2560 | tf_op jit(solution)/shard_map/all_gather | solution.py:35
  202.4 7.7 %all-gather.10 = f32[4,1,128]{2,1,0:T(1,128)S(1)} all-gather(f32[1,1,128]{2,1,0:T(1,128)S(1)} %bitcast.82), channel_id=4, replica_groups=mesh['lat_0'=4,'lat_1'=2,'lon_0'=4,'lon_1'=4] {'lon_1'}, dimensions={0}, use_global_device_ids=true | all-gather | bytes 2560 | tf_op jit(solution)/shard_map/all_gather | solution.py:35
  210.1 0.7 cosine_reduce_fusion
  211.5 0.0 collective-permute-done.1
  211.5 0.7 copy-done.1
  212.2 1.0 pad_maximum_fusion.1
  213.3 10.8 %gather_fusion = bf16[512,128,128]{1,2,0:T(8,128)(2,1)} fusion(bf16[10,2,128,128]{2,3,0,1:T(8,128)(2,1)S(1)} %pad_maximum_fusion.1, s32[512]{0:T(512)S(1)} %reshape.258), kind=kCustom, calls=%fused_computation | custom fusion | bytes 33558528 | tf_op jit(solution)/shard_map/gather | solution.py:78
  224.1 0.0 collective-permute-done.4
  224.1 3.3 %bitcast_dynamic-update-slice_fusion.4 = bf16[72,5,128,128]{2,3,0,1:T(8,128)(2,1)} fusion(bf16[72,128,128]{1,2,0:T(8,128)(2,1)} %collective-permute-done.4), kind=kLoop, calls=%fused_computation.18 | loop fusion | bytes 4718592
  227.4 0.0 collective-permute-done.5
  227.4 3.4 %bitcast_dynamic-update-slice_fusion.3 = bf16[72,5,128,128]{2,3,0,1:T(8,128)(2,1)} fusion(bf16[72,5,128,128]{2,3,0,1:T(8,128)(2,1)} %bitcast_dynamic-update-slice_fusion.4, bf16[72,128,128]{1,2,0:T(8,128)(2,1)} %collective-permute-done.5), kind=kLoop, calls=%fused_computation.17 | loop fusion | bytes 4718592
  230.8 1.7 bitcast_dynamic-update-slice_fusion.2
  232.5 0.0 collective-permute-done.6
  232.5 3.4 %bitcast_dynamic-update-slice_fusion.1 = bf16[72,5,128,128]{2,3,0,1:T(8,128)(2,1)} fusion(bf16[72,5,128,128]{2,3,0,1:T(8,128)(2,1)} %bitcast_dynamic-update-slice_fusion.2, bf16[72,128,128]{1,2,0:T(8,128)(2,1)} %collective-permute-done.6), kind=kLoop, calls=%fused_computation.15 | loop fusion | bytes 4718592
  235.9 0.0 collective-permute-done.7
  235.9 3.4 %bitcast_dynamic-update-slice_fusion = bf16[72,5,128,128]{2,3,0,1:T(8,128)(2,1)} fusion(bf16[72,5,128,128]{2,3,0,1:T(8,128)(2,1)} %bitcast_dynamic-update-slice_fusion.1, bf16[72,128,128]{1,2,0:T(8,128)(2,1)} %collective-permute-done.7), kind=kLoop, calls=%fused_computation.14 | loop fusion | bytes 4718592 | tf_op jit(solution)/shard_map/stack | solution.py:68
  239.3 15.2 %gather_fusion.1 = bf16[512,128,128]{1,2,0:T(8,128)(2,1)} fusion(bf16[72,5,128,128]{2,3,0,1:T(8,128)(2,1)} %bitcast_dynamic-update-slice_fusion, s32[512]{0:T(512)S(1)} %reshape.264), kind=kCustom, calls=%fused_computation.1 | custom fusion | bytes 33558528 | tf_op jit(solution)/shard_map/gather | solution.py:69
  254.5 19.4 %fusion.7 = (f32[128]{0:T(128)S(1)}, f32[64,128,128,1]{2,1,3,0:T(8,128)}) fusion(f32[64]{0:T(128)S(1)} %add_cosine_fusion, bf16[64,1,8,128,128]{4,3,2,1,0:T(8,128)(2,1)} %param.6, bf16[64,8,128,128]{2,3,1,0:T(8,128)(2,1)} %bitcast.73, bf16[64,8,128,128]{2,3,1,0:T(8,128)(2,1)} %bitcast.74, pred[64,8]{1,0:T(8,128)(4,1)S(1)} %copy.14, pred[64,8]{1,0:T(8,128)(4,1)S(1)} %copy.12), kind=kOutput, calls=%fused_computation.11 | convolution fusion | flops 2166358016 | bytes 54527744 | tf_op jit(solution)/shard_map/tkij,tkjc->tic/dot_general | solution.py:88
  273.9 7.9 %all-gather.11 = f32[4,1,128]{2,1,0:T(1,128)S(1)} all-gather(f32[1,1,128]{2,1,0:T(1,128)S(1)} %bitcast.86), channel_id=5, replica_groups=mesh['lat_0'=4,'lat_1'=2,'lon_0'=4,'lon_1'=4] {'lat_0'}, dimensions={0}, use_global_device_ids=true | all-gather | bytes 2560 | tf_op jit(solution)/shard_map/all_gather | solution.py:35
  281.8 1.8 all-gather.12
  283.6 8.6 %all-gather.13 = f32[4,1,128]{2,1,0:T(1,128)S(1)} all-gather(f32[1,1,128]{2,1,0:T(1,128)S(1)} %bitcast.83), channel_id=7, replica_groups=mesh['lat_0'=4,'lat_1'=2,'lon_0'=4,'lon_1'=4] {'lon_0'}, dimensions={0}, use_global_device_ids=true | all-gather | bytes 2560 | tf_op jit(solution)/shard_map/all_gather | solution.py:35
  292.2 8.3 %all-gather.14 = f32[4,1,128]{2,1,0:T(1,128)S(1)} all-gather(f32[1,1,128]{2,1,0:T(1,128)S(1)} %bitcast.84), channel_id=8, replica_groups=mesh['lat_0'=4,'lat_1'=2,'lon_0'=4,'lon_1'=4] {'lon_1'}, dimensions={0}, use_global_device_ids=true | all-gather | bytes 2560 | tf_op jit(solution)/shard_map/all_gather | solution.py:35
  300.5 4.9 %bitcast_add_fusion = f32[64,128,128]{2,1,0:T(8,128)} fusion(f32[64,128,128,1]{2,1,3,0:T(8,128)} %get-tuple-element.14, f32[128]{0:T(128)S(1)} %subtract_divide_fusion), kind=kLoop, calls=%fused_computation.9 | loop fusion | flops 1048576 | bytes 8389120 | tf_op jit(solution)/shard_map/add | solution.py:93
  (22 shorter events, 0.3 us)
Async XLA Ops:
  0.0 19.4 %copy-start = (bf16[64,128,32,4]{1,3,2,0:T(4,128)(2,1)S(1)}, bf16[64,128,32,4]{1,3,2,0:T(4,128)(2,1)}, u32[]{:S(2)}) copy-start(bf16[64,128,32,4]{1,3,2,0:T(4,128)(2,1)} %param.5) | copy-start | bytes 6291460
  0.0 20.7 %copy-start.2 = (s32[64,1,8]{0,2,1:T(8,128)S(1)}, s32[64,1,8]{0,2,1:T(8,128)}, u32[]{:S(2)}) copy-start(s32[64,1,8]{0,2,1:T(8,128)} %param.8) | copy-start | bytes 6148
  0.0 20.7 %copy-start.4 = (s32[64,1]{0,1:T(1,128)S(1)}, s32[64,1]{0,1:T(1,128)}, u32[]{:S(2)}) copy-start(s32[64,1]{0,1:T(1,128)} %param.9) | copy-start | bytes 772
  0.0 20.7 %copy-start.3 = (s32[64,1,8]{0,2,1:T(8,128)S(1)}, s32[64,1,8]{0,2,1:T(8,128)}, u32[]{:S(2)}) copy-start(s32[64,1,8]{0,2,1:T(8,128)} %param.7) | copy-start | bytes 6148
  1.2 2.6 collective-permute-start.2
  2.5 5.1 %collective-permute-start.3 = (bf16[4,128,128]{1,2,0:T(8,128)(2,1)S(1)}, bf16[4,128,128]{1,2,0:T(8,128)(2,1)S(1)}, u32[]{:S(2)}, u32[]{:S(2)}) collective-permute-start(bf16[4,128,128]{1,2,0:T(8,128)(2,1)S(1)} %bitcast.79), channel_id=1, source_target_pairs={{16,0},{32,16},{48,32},{64,48},{80,64},{96,80},{112,96},{17,1},{33... | collective-permute-start | bytes 393224 | tf_op jit(solution)/shard_map/ppermute | solution.py:23
  10.9 213.2 %collective-permute-start.4 = (bf16[72,128,128]{1,2,0:T(8,128)(2,1)}, bf16[72,128,128]{1,2,0:T(8,128)(2,1)}, u32[]{:S(2)}, u32[]{:S(2)}) collective-permute-start(bf16[72,128,128]{1,2,0:T(8,128)(2,1)} %pad_maximum_fusion), channel_id=1, source_target_pairs={{0,2},{1,3},{2,4},{3,5},{4,6},{5,7},{6,8},{7,9},{8,10},{9,11},{10,... | collective-permute-start | bytes 7077896 | tf_op jit(solution)/shard_map/ppermute | solution.py:30
  14.1 213.3 %collective-permute-start.5 = (bf16[72,128,128]{1,2,0:T(8,128)(2,1)}, bf16[72,128,128]{1,2,0:T(8,128)(2,1)}, u32[]{:S(2)}, u32[]{:S(2)}) collective-permute-start(bf16[72,128,128]{1,2,0:T(8,128)(2,1)} %pad_maximum_fusion), channel_id=1, source_target_pairs={{0,1},{1,2},{2,3},{3,4},{4,5},{5,6},{6,7},{7,8},{8,9},{9,10},{10,1... | collective-permute-start | bytes 7077896 | tf_op jit(solution)/shard_map/ppermute | solution.py:30
  14.8 217.8 %collective-permute-start.6 = (bf16[72,128,128]{1,2,0:T(8,128)(2,1)}, bf16[72,128,128]{1,2,0:T(8,128)(2,1)}, u32[]{:S(2)}, u32[]{:S(2)}) collective-permute-start(bf16[72,128,128]{1,2,0:T(8,128)(2,1)} %pad_maximum_fusion), channel_id=1, source_target_pairs={{0,15},{1,0},{2,1},{3,2},{4,3},{5,4},{6,5},{7,6},{8,7},{9,8},{10,9... | collective-permute-start | bytes 7077896 | tf_op jit(solution)/shard_map/ppermute | solution.py:30
  19.6 216.3 %collective-permute-start.7 = (bf16[72,128,128]{1,2,0:T(8,128)(2,1)}, bf16[72,128,128]{1,2,0:T(8,128)(2,1)}, u32[]{:S(2)}, u32[]{:S(2)}) collective-permute-start(bf16[72,128,128]{1,2,0:T(8,128)(2,1)} %pad_maximum_fusion), channel_id=1, source_target_pairs={{0,14},{1,15},{2,0},{3,1},{4,2},{5,3},{6,4},{7,5},{8,6},{9,7},{10,... | collective-permute-start | bytes 7077896 | tf_op jit(solution)/shard_map/ppermute | solution.py:30
  20.6 155.7 %collective-permute-start = (bf16[10,128,128]{1,2,0:T(8,128)(2,1)S(1)}, bf16[10,128,128]{1,2,0:T(8,128)(2,1)S(1)}, u32[]{:S(2)}, u32[]{:S(2)}) collective-permute-start(bf16[10,128,128]{1,2,0:T(8,128)(2,1)S(1)} %pad_maximum_fusion.2), channel_id=1, source_target_pairs={{0,3},{1,4},{2,5},{3,6},{4,7},{5,8},{6,9},{7,10},{8,11},{9,12},{10... | collective-permute-start | bytes 983048 | tf_op jit(solution)/shard_map/ppermute | solution.py:30
  176.2 35.3 %collective-permute-start.1 = (bf16[10,128,128]{1,2,0:T(8,128)(2,1)S(1)}, bf16[10,128,128]{1,2,0:T(8,128)(2,1)S(1)}, u32[]{:S(2)}, u32[]{:S(2)}) collective-permute-start(bf16[10,128,128]{1,2,0:T(8,128)(2,1)S(1)} %pad_maximum_fusion.2), channel_id=1, source_target_pairs={{0,13},{1,14},{2,15},{3,0},{4,1},{5,2},{6,3},{7,4},{8,5},{9,6},{10... | collective-permute-start | bytes 983048 | tf_op jit(solution)/shard_map/ppermute | solution.py:30
  211.5 0.7 copy-start.1
